TPU v7x, 8 devices: a whole 2x2x1 slice. The times are simulated.
8 devices in a mesh: dp: 1 (over z), tp: 8 (over y, x, core).
Axes of the slice: x: 2, y: 2, z: 1, core: 2. Of those that a mesh axis runs over, the one named last changes fastest.
Arguments:
- hidden: bfloat16 [8, 9, 4096], P('dp')
- draft_ids: int32 [8, 8], P('dp')
- norm_gain: bfloat16 [4096], replicated
- head_w: bfloat16 [4096, 128256], P(None, 'tp')
Outputs:
- output 1: float32 [8, 8], P('dp')
- output 2: float32 [8, 9], P('dp')
- output 3: float32 [8, 9], P('dp')
All inputs are finite; a program needn't handle non-finite values.
Results may differ from a plain program's by a relative error of at most 0.001.
Values sent between devices are 32-bit elements.
A program may use at most 1 GiB of HBM per device.

v0:
```python
import jax
import jax.numpy as jnp
from jax import lax
from jax.sharding import PartitionSpec as P

NORM_EPS = 1e-5


def rms_norm(hidden, norm_gain):
    wide_x = hidden.astype(jnp.float32)
    inv_rms = lax.rsqrt(jnp.mean(wide_x * wide_x, axis=-1, keepdims=True) + NORM_EPS)
    return (wide_x * inv_rms * norm_gain.astype(jnp.float32)).astype(jnp.bfloat16)


def solution(mesh):
    def per_device(hidden, draft_ids, norm_gain, head_w):
        normed = rms_norm(hidden, norm_gain)
        logits = jnp.einsum('btd,dv->btv', normed, head_w, preferred_element_type=jnp.float32)
        gathered = lax.all_gather(logits, 'tp')
        shards = gathered.shape[0]
        shard_cols = gathered.shape[3]
        drafts = draft_ids.shape[1]
        row_max = jnp.max(gathered, axis=(0, 3))
        shifted = gathered - row_max[None, :, :, None]
        exp_vals = jnp.exp(shifted)
        exp_sum = jnp.sum(exp_vals, axis=(0, 3))
        weighted = jnp.sum(exp_vals * shifted, axis=(0, 3))
        log_sum = jnp.log(exp_sum)
        log_norm = row_max + log_sum
        entropy = log_sum - weighted / exp_sum
        col_ids = lax.broadcasted_iota(jnp.int32, (shards, 1, 1, shard_cols), 0) * shard_cols + lax.broadcasted_iota(jnp.int32, (shards, 1, 1, shard_cols), 3)
        picked = jnp.sum(jnp.where(col_ids == draft_ids[None, :, :, None], gathered[:, :, :drafts], 0.0), axis=(0, 3))
        return picked - log_norm[:, :drafts], log_norm, entropy

    specs_in = (P('dp', None, None), P('dp', None), P(None), P(None, 'tp'))
    specs_out = (P('dp', None), P('dp', None), P('dp', None))
    return jax.shard_map(per_device, mesh=mesh, in_specs=specs_in, out_specs=specs_out, check_vma=False)
```

profile of v0, /device:TPU:0, one launch (start us, length us, event | category | flops | bytes accessed | tf_op | source)
XLA Modules:
  0.0 290.4 jit_solution(13528815816662992547)
XLA Ops:
  7.2 0.0 all-gather.3.cloned.1.call-start
  7.2 1.3 fusion.4
  8.5 0.7 convert_element_type.10
  9.2 0.0 copy-start
  9.2 50.5 %fusion = f32[8,9,16032]{2,0,1:T(8,128)} fusion(bf16[4096,16032]{0,1:T(8,128)(2,1)} %param.7, bf16[8,9,4096]{2,0,1:T(8,128)(2,1)} %param.4, f32[4096]{0:T(1024)S(1)} %convert_element_type.10, f32[8,9]{0,1:T(8,128)S(1)} %add_rsqrt_fusion), kind=kOutput, calls=%fused_computation | convolution fusion | flops 9457238016 | bytes 136557856 | tf_op jit(solution)/shard_map/btd,dv->btv/dot_general | solution.py:18
  59.7 0.0 all-gather.3.cloned.1.call-update
  59.7 0.0 copy-done
  59.7 0.1 copy.18
  59.8 0.1 iota_add_fusion
  59.9 174.3 %all-gather.3.cloned.1.call-done = f32[64,9,16032]{2,0,1:T(8,128)} async-done(((f32[8,9,16032]{2,0,1:T(8,128)}), f32[64,9,16032]{2,0,1:T(8,128)}) %all-gather.3.cloned.1.call-update) | async-done | bytes 36937744 | tf_op jit(solution)/shard_map/all_gather | solution.py:19
  234.2 13.5 %reduce = f32[64,9]{0,1:T(8,128)S(1)} reduce(f32[64,9,16032]{2,0,1:T(8,128)} %all-gather.3.cloned.1.call-done, f32[]{:T(128)} %constant.10.clone.1), dimensions={2}, to_apply=%region_2.0 | reduce | flops 9233856 | bytes 36940036 | tf_op jit(solution)/shard_map/reduce_max | solution.py:23
  247.7 0.1 reshape.32
  247.8 20.5 %fusion.2 = (f32[8,9]{0,1:T(8,128)S(1)}, f32[8,9]{0,1:T(8,128)S(1)}) fusion(f32[8,9]{0,1:T(8,128)S(1)} %reduce_max.9, f32[64,9,16032]{2,0,1:T(8,128)} %all-gather.3.cloned.1.call-done), kind=kLoop, calls=%fused_computation.4 | loop fusion | flops 36937584 | bytes 36938592 | tf_op jit(solution)/shard_map/reduce_sum | solution.py:27
  268.4 0.7 copy.22
  269.0 13.1 %fusion.3 = f32[8,8]{0,1:T(8,128)S(1)} fusion(f32[8,8,9,16032]{3,1,0,2:T(8,128)} %bitcast.9, s32[8,8]{0,1:T(8,128)S(1)} %copy.18, s32[8,16032]{1,0:T(8,128)S(1)} %iota_add_fusion), kind=kLoop, calls=%fused_computation.6 | loop fusion | flops 24625088 | bytes 33347072 | tf_op jit(solution)/shard_map/reduce_sum | solution.py:32
  282.2 0.7 copy.21
  282.8 0.7 copy.23
  (5 shorter events, 0.0 us)
Async XLA Ops:
  7.2 227.0 %all-gather.3.cloned.1.call-start = ((), (), s32[]{:S(2)}) async-start(), calls=%async_computation | async-start | bytes 41803776 | tf_op jit(solution)/shard_map/all_gather | solution.py:19
  9.2 50.5 %copy-start = (s32[8,8]{1,0:T(8,128)S(1)}, s32[8,8]{1,0:T(8,128)}, u32[]{:S(2)}) copy-start(s32[8,8]{1,0:T(8,128)} %param.5) | copy-start | bytes 772
Sparse Core Ops, SparseCore 0:
  59.8 174.3 all-gather.2
where the time goes:
time: 291 us; the launch traced here: 290 us
  waiting for transfers between devices  174 us (60%)
  matrix products  50.5 us (17%)
  other arithmetic  49.3 us (17%)
  between operations  14.1 us (5%)
    all_gather x1, waiting for transfers between devices, per_device(): gathered = lax.all_gather(logits, 'tp')  174 us
    dot_general x1, matrix products, per_device(): jnp.einsum('btd,dv->btv', normed, head_w, preferred_element_type=jnp.floa...  50.5 us
    reduce_sum x1, other arithmetic, per_device(): weighted = jnp.sum(exp_vals * shifted, axis=(0, 3))  20.5 us
    reduce_max x2, other arithmetic, per_device(): row_max = jnp.max(gathered, axis=(0, 3))  13.5 us
    reduce_sum x1, other arithmetic, per_device(): jnp.sum(jnp.where(col_ids == draft_ids[None, :, :, None], gathered[:, :,...  13.1 us
  transfers between devices with their start and end apart: 1, of which 1 were waited for; matrix products, arithmetic and copies ran while one was open for 0% of the time, Pallas kernels for 0%

commit v1 on v0

v1 whole, which is shorter than its diff:
```python
import functools

import jax
import jax.numpy as jnp
from jax import lax
from jax.experimental import pallas as pl
from jax.experimental.pallas import tpu as pltpu
from jax.sharding import PartitionSpec as P

NORM_EPS = 1e-5
MESH = pl.DeviceIdType.MESH
LANES = 128
SUBLANES = 8
BLOCK = 256
SLOTS = 16
UNROLL = 4


def merge(state, logits, wanted):
    row_max, exp_sum, weighted, picked = state
    tiles = logits.reshape(-1, SUBLANES, LANES)
    new_max = jnp.maximum(row_max, jnp.max(tiles, axis=0))
    drop = row_max - new_max
    scale = jnp.exp(drop)
    shifted = tiles - new_max[None]
    exp_vals = jnp.exp(shifted)
    weighted = scale * (weighted + drop * exp_sum) + jnp.sum(exp_vals * shifted, axis=0)
    exp_sum = scale * exp_sum + jnp.sum(exp_vals, axis=0)
    steps = lax.broadcasted_iota(jnp.int32, tiles.shape, 0) * SUBLANES
    picked = picked + jnp.sum(jnp.where(wanted[None] == steps, tiles, 0.0), axis=0)
    return new_max, exp_sum, weighted, picked


def kernel(n, x_hbm, ids_ref, gain_ref, w_hbm, logp_ref, norm_ref, ent_ref,
           x_ref, xt_ref, w_ref, stats_ref, x_sem, w_sem, send_sem, recv_sem):
    me = lax.axis_index('tp')
    group = lax.axis_index('dp')
    batch, drafts = ids_ref.shape
    positions = norm_ref.shape[1]
    rows = batch * positions
    cols, dim = w_hbm.shape
    full = cols // BLOCK
    tail = cols - full * BLOCK

    def fetch(block, slot, size=BLOCK):
        start = pl.multiple_of(block * BLOCK, BLOCK)
        return pltpu.make_async_copy(w_hbm.at[pl.ds(start, size)], w_ref.at[slot, pl.ds(0, size)], w_sem.at[slot])

    x_copy = pltpu.make_async_copy(x_hbm, x_ref, x_sem)
    x_copy.start()
    for b in range(SLOTS):
        fetch(b, b).start()

    barrier = pltpu.get_barrier_semaphore()
    for o in range(1, n):
        pl.semaphore_signal(barrier, inc=1, device_id=(group, lax.rem(me + o, n)), device_id_type=MESH)

    lane = lax.broadcasted_iota(jnp.int32, (batch, LANES), 1)
    sub = lax.broadcasted_iota(jnp.int32, (batch, LANES), 0)
    ids = ids_ref[...]
    spread = jnp.full((batch, LANES), 0, jnp.int32)
    for t in range(drafts):
        spread = jnp.where((lane // batch) == t, ids[:, t:t + 1], spread)
    spread = jnp.sum(jnp.where(lane % batch == sub, spread, 0), axis=0, keepdims=True)
    wanted = jnp.where(lane < batch * drafts, spread - me * cols - sub, -(1 << 29))

    x_copy.wait()
    total = jnp.zeros((rows, LANES), jnp.float32)
    for c in range(dim // LANES):
        wide = x_ref[:, c * LANES:(c + 1) * LANES].astype(jnp.float32)
        total = total + wide * wide
    inv_rms = lax.rsqrt(jnp.sum(total, axis=1, keepdims=True) / dim + NORM_EPS)
    pad = jnp.zeros((LANES - rows, LANES), jnp.float32)
    gain = gain_ref[...].astype(jnp.float32)
    for c in range(dim // LANES):
        wide = x_ref[:, c * LANES:(c + 1) * LANES].astype(jnp.float32)
        normed = wide * inv_rms * gain[c:c + 1, :]
        padded = jnp.concatenate([normed, pad], axis=0)
        xt_ref[c * LANES:(c + 1) * LANES, :] = padded.T.astype(jnp.bfloat16)

    def step(block, slot, state, first, size=BLOCK):
        fetch(block, slot, size).wait()
        logits = jnp.dot(w_ref[slot, :size], xt_ref[...], preferred_element_type=jnp.float32)
        if first:
            top = jnp.max(logits.reshape(-1, SUBLANES, LANES), axis=0)
            zero = jnp.zeros((SUBLANES, LANES), jnp.float32)
            state = (top, zero, zero, zero)
        return merge(state, logits, wanted - block * BLOCK)

    def again(block, slot):
        @pl.when(block + SLOTS < full)
        def _():
            fetch(block + SLOTS, slot).start()
        if tail:
            @pl.when(block + SLOTS == full)
            def _():
                fetch(full, slot, tail).start()

    state = step(0, 0, None, True)
    again(0, 0)
    head = 1
    trips = (full - head) // UNROLL

    def body(i, state):
        for u in range(UNROLL):
            block = head + i * UNROLL + u
            slot = lax.rem(block, SLOTS)
            state = step(block, slot, state, False)
            again(block, slot)
        return state

    state = lax.fori_loop(0, trips, body, state)
    for block in range(head + trips * UNROLL, full):
        state = step(block, block % SLOTS, state, False)
        if block + SLOTS <= full:
            again(block, block % SLOTS)
    if tail:
        state = step(full, full % SLOTS, state, False, tail)

    row_max, exp_sum, weighted, picked = state
    top = jnp.max(row_max, axis=0, keepdims=True)
    drop = row_max - top
    scale = jnp.exp(drop)
    mine = [top, jnp.sum(scale * exp_sum, axis=0, keepdims=True),
            jnp.sum(scale * (weighted + drop * exp_sum), axis=0, keepdims=True), jnp.sum(picked, axis=0, keepdims=True)]
    sub8 = lax.broadcasted_iota(jnp.int32, (SUBLANES, LANES), 0)
    packed = jnp.zeros((SUBLANES, LANES), jnp.float32)
    for k, v in enumerate(mine):
        packed = jnp.where(sub8 == k, v, packed)
    stats_ref[me] = packed
    pl.semaphore_wait(barrier, n - 1)
    copies = []
    for o in range(1, n):
        peer = lax.rem(me + o, n)
        copy = pltpu.make_async_remote_copy(
            src_ref=stats_ref.at[me], dst_ref=stats_ref.at[me], send_sem=send_sem.at[o], recv_sem=recv_sem.at[o],
            device_id=(group, peer), device_id_type=MESH)
        copy.start()
        copies.append(copy)
    for copy in copies:
        copy.wait()

    every = stats_ref[...]
    top = jnp.max(every[:, 0:1], axis=0)
    drop = every[:, 0:1] - top[None]
    scale = jnp.exp(drop)
    exp_sum = jnp.sum(scale * every[:, 1:2], axis=0)
    weighted = jnp.sum(scale * (every[:, 2:3] + drop * every[:, 1:2]), axis=0)
    picked = jnp.sum(every[:, 3:4], axis=0)
    log_sum = jnp.log(exp_sum)
    log_norm = top + log_sum
    entropy = log_sum - weighted / exp_sum
    logp = picked - log_norm

    def unspread(values, width):
        out = jnp.zeros((batch, LANES), jnp.float32)
        wide = jnp.broadcast_to(values, (batch, LANES))
        for t in range(width):
            out = jnp.where(lane == t, jnp.sum(jnp.where(lane == t * batch + sub, wide, 0.0), axis=1, keepdims=True), out)
        return out[:, :width]

    logp_ref[...] = unspread(logp, drafts)
    norm_ref[...] = unspread(log_norm, positions)
    ent_ref[...] = unspread(entropy, positions)


def solution(mesh):
    n = mesh.shape['tp']

    def per_device(hidden, draft_ids, norm_gain, head_w):
        batch, positions, dim = hidden.shape
        drafts = draft_ids.shape[1]
        rows = batch * positions
        x = hidden.transpose(1, 0, 2).reshape(rows, dim)
        gain = norm_gain.reshape(dim // LANES, LANES)
        vmem = pl.BlockSpec(memory_space=pltpu.VMEM)
        hbm = pl.BlockSpec(memory_space=pltpu.HBM)
        return pl.pallas_call(
            functools.partial(kernel, n),
            out_shape=(jax.ShapeDtypeStruct((batch, drafts), jnp.float32),
                       jax.ShapeDtypeStruct((batch, positions), jnp.float32),
                       jax.ShapeDtypeStruct((batch, positions), jnp.float32)),
            in_specs=[hbm, vmem, vmem, hbm],
            out_specs=(vmem, vmem, vmem),
            scratch_shapes=[
                pltpu.VMEM((rows, dim), jnp.bfloat16),
                pltpu.VMEM((dim, LANES), jnp.bfloat16),
                pltpu.VMEM((SLOTS, BLOCK, dim), jnp.bfloat16),
                pltpu.VMEM((n, SUBLANES, LANES), jnp.float32),
                pltpu.SemaphoreType.DMA,
                pltpu.SemaphoreType.DMA((SLOTS,)),
                pltpu.SemaphoreType.DMA((n,)),
                pltpu.SemaphoreType.DMA((n,)),
            ],
            compiler_params=pltpu.CompilerParams(collective_id=0, has_side_effects=True, vmem_limit_bytes=60 * 1024 * 1024),
        )(x, draft_ids, gain, head_w.T)

    specs_in = (P('dp', None, None), P('dp', None), P(None), P(None, 'tp'))
    specs_out = (P('dp', None), P('dp', None), P('dp', None))
    return jax.shard_map(per_device, mesh=mesh, in_specs=specs_in, out_specs=specs_out, check_vma=False)
```

time: 291 us -> 70 us (0.24)
  waiting for transfers between devices: 174 us -> 0 us
  Pallas kernels: 0 us -> 65.3 us
  matrix products: 50.5 us -> 0 us
  other arithmetic: 49.3 us -> 0 us
  between operations: 14.1 us -> 0.64 us
    all_gather x1 -> x0, waiting for transfers between devices: 174 us -> none  [per_device(): gathered = lax.all_gather(logits, 'tp')]
    pallas_call x0 -> x1, Pallas kernels: none -> 65.3 us  [per_device(): pl.pallas_call(functools.partial(kernel, n), out_shape=(jax.ShapeDtypeStr...]
    dot_general x1 -> x0, matrix products: 50.5 us -> none  [per_device(): jnp.einsum('btd,dv->btv', normed, head_w, preferred_element_type=jnp.floa...]
    reduce_sum x3 -> x0, other arithmetic: 34.9 us -> none  [the longest x1 20.5 us: per_device(): weighted = jnp.sum(exp_vals * shifted, axis=(0, 3))]
    reduce_max x2 -> x0, other arithmetic: 13.5 us -> none  [per_device(): row_max = jnp.max(gathered, axis=(0, 3))]
  transfers between devices with their start and end apart: 1 -> 0, of which waited for: 1 -> 0; matrix products, arithmetic and copies ran while one was open for 0% -> 0% of each run, Pallas kernels for 0% -> 0%
where the time goes in v1:
time: 70 us; the launch traced here: 69.7 us
  Pallas kernels  65.3 us (93%)
  local copies, waits for them, and re-layouts  3.8 us (5%)
    pallas_call x1, Pallas kernels, per_device(): pl.pallas_call(functools.partial(kernel, n), out_shape=(jax.ShapeDtypeStr...  65.3 us
    unnamed x3, local copies, waits for them, and re-layouts  3.8 us

profile of v1, /device:TPU:0, one launch (start us, length us, event | category | flops | bytes accessed | tf_op | source)
XLA Modules:
  0.0 69.7 jit_solution(12904998087047468792)
XLA Ops:
  0.6 65.3 %shard_map.67 = (f32[8,8]{1,0:T(8,128)}, f32[8,9]{1,0:T(8,128)}, f32[8,9]{1,0:T(8,128)}) custom-call(bf16[72,4096]{1,0:T(8,128)(2,1)} %bitcast.5, s32[8,8]{1,0:T(8,128)} %ids_ref.1, bf16[32,128]{1,0:T(8,128)(2,1)} %bitcast.6, bf16[16032,4096]{1,0:T(8,128)(2,1)} %bitcast.3.w_hbm), custom_call_target="tpu_custom_call" | custom-call | tf_op jit(solution)/shard_map/pallas_call | solution.py:178
  65.9 1.3 %copy.10 = f32[8,8]{1,0:T(8,128)} copy(f32[8,8]{1,0:T(8,128)} %get-tuple-element.6) | data formatting | bytes 512
  67.2 1.3 %copy.11 = f32[8,9]{1,0:T(8,128)} copy(f32[8,9]{1,0:T(8,128)} %get-tuple-element.7) | data formatting | bytes 576
  68.4 1.3 %copy.12 = f32[8,9]{1,0:T(8,128)} copy(f32[8,9]{1,0:T(8,128)} %get-tuple-element.8) | data formatting | bytes 576

commit v2 on v0

v2 whole, which is shorter than its diff:
```python
import functools

import jax
import jax.numpy as jnp
from jax import lax
from jax.experimental import pallas as pl
from jax.experimental.pallas import tpu as pltpu
from jax.sharding import PartitionSpec as P

NORM_EPS = 1e-5
MESH = pl.DeviceIdType.MESH
LANES = 128
SUBLANES = 8
UNIT = 256
PACK = 16
HELD = 256
MOVED = 304
UNITS = 2
TRIP = UNITS * (HELD + MOVED)
SLOTS = 5
CUTS = 4
FIELD = 16


def fold(state, tiles, hits, start):
    row_max, exp_sum, weighted, picked = state
    base = row_max if start is None else jnp.where(start, tiles[0], row_max)
    new_max = functools.reduce(jnp.maximum, tiles, base)
    drop = base - new_max
    scale = jnp.exp(drop)
    weighted = scale * (weighted + drop * exp_sum)
    exp_sum = scale * exp_sum
    for tile, hit in zip(tiles, hits):
        shifted = tile - new_max
        exp_vals = jnp.exp(shifted)
        exp_sum = exp_sum + exp_vals
        weighted = weighted + exp_vals * shifted
        picked = picked + jnp.where(hit, tile, 0.0)
    return new_max, exp_sum, weighted, picked


def score(x_hbm, ids_ref, gain_ref, w_hbm, stats_ref,
          x_ref, n_ref, xt_ref, w_ref, edge_ref, state_ref, x_sem, w_sem, edge_sem, cut_sem):
    me = lax.axis_index('tp')
    batch, drafts = ids_ref.shape
    rows = x_hbm.shape[0]
    positions = rows // batch
    cols, dim = w_hbm.shape
    depth = dim // UNIT
    trips = cols // TRIP
    edge = cols - trips * TRIP
    cut = dim // CUTS

    def fetch(trip, slot):
        start = pl.multiple_of(edge + trip * TRIP, SUBLANES)
        return pltpu.make_async_copy(w_hbm.at[pl.ds(start, TRIP)], w_ref.at[slot], w_sem.at[slot])

    def fetch_cut(c):
        part = pl.ds(c * cut, cut)
        return pltpu.make_async_copy(w_hbm.at[pl.ds(cols - TRIP, TRIP), part], w_ref.at[(trips - 1) % SLOTS, :, part], cut_sem.at[c])

    x_copy = pltpu.make_async_copy(x_hbm, x_ref, x_sem)
    x_copy.start()
    edge_copy = pltpu.make_async_copy(w_hbm.at[pl.ds(0, edge)], edge_ref, edge_sem)
    edge_copy.start()
    for b in range(SLOTS):
        fetch(b, b).start()

    lane = lax.broadcasted_iota(jnp.int32, (SUBLANES, LANES), 1)
    sub = lax.broadcasted_iota(jnp.int32, (SUBLANES, LANES), 0)
    ids = ids_ref[...] - me * cols
    nobody = jnp.full((SUBLANES, LANES), -(1 << 29), jnp.int32)
    wide_ids = [ids[:, t:t + 1] - lane for t in range(drafts)] + [nobody] * (positions - drafts)
    tall_ids = nobody
    for t in range(drafts):
        spread = jnp.sum(jnp.where(lane == t * batch + sub, ids[:, t:t + 1], 0), axis=0, keepdims=True)
        tall_ids = jnp.where(lane // batch == t, spread - sub, tall_ids)

    x_copy.wait()
    total = jnp.zeros((rows, LANES), jnp.float32)
    for c in range(dim // LANES):
        wide = x_ref[:, c * LANES:(c + 1) * LANES].astype(jnp.float32)
        total = total + wide * wide
    inv_rms = lax.rsqrt(jnp.sum(total, axis=1, keepdims=True) / dim + NORM_EPS)
    gain = gain_ref[...].astype(jnp.float32)
    pad = jnp.zeros((LANES - rows, LANES), jnp.float32)
    for c in range(dim // LANES):
        wide = x_ref[:, c * LANES:(c + 1) * LANES].astype(jnp.float32)
        normed = jnp.concatenate([wide * inv_rms * gain[c:c + 1, :], pad], axis=0)
        n_ref[:, c * LANES:(c + 1) * LANES] = normed[:n_ref.shape[0]].astype(jnp.bfloat16)
        xt_ref[c * LANES:(c + 1) * LANES, :] = normed.T.astype(jnp.bfloat16)

    zeros = jnp.zeros((UNIT, UNIT - LANES), jnp.bfloat16)

    def hold_x(k, q):
        pltpu.matmul_push_rhs(jnp.concatenate([xt_ref[k * UNIT:(k + 1) * UNIT, :], zeros], axis=1), staging_register=1, mxu_index=q)

    def tall_tiles(logits):
        return [logits[r:r + SUBLANES, :LANES] for r in range(0, logits.shape[0], SUBLANES)]

    def tall_hits(first_row, count):
        return [(tall_ids - first_row) == r * SUBLANES for r in range(count)]

    def main(held_0, held_1, moved_0, moved_1, edge_0, edge_1):
        held, moved, edges = (held_0, held_1), (moved_0, moved_1), (edge_0, edge_1)
        for ref in held + moved + edges:
            pltpu.matmul_pop(ref)

        half = edge // UNITS
        for q in range(UNITS):
            hold_x(0, q)
        edge_copy.wait()
        for k in range(depth):
            for q in range(UNITS):
                pltpu.matmul_acc_lhs(edges[q], edge_ref[q * half:(q + 1) * half, k * UNIT:(k + 1) * UNIT], load_staged_rhs=1)
                hold_x((k + 1) % depth, q)
        tiles, hits = [], []
        for q in range(UNITS):
            tiles += tall_tiles(pltpu.matmul_pop(edges[q]))
            hits += tall_hits(q * half, half // SUBLANES)
        zero = jnp.zeros((SUBLANES, LANES), jnp.float32)
        tall = fold((tiles[0], zero, zero, zero), tiles, hits, None)
        state_ref[...] = jnp.zeros_like(state_ref)

        def trip_step(trip, slot, tall, last):
            if not last:
                fetch(trip, slot).wait()
            first_row = edge + trip * TRIP
            for k in range(depth):
                if last and k % (depth // CUTS) == 0:
                    fetch_cut(k // (depth // CUTS)).wait()
                part = slice(k * UNIT, (k + 1) * UNIT)
                for q in range(UNITS):
                    top = q * (HELD + MOVED)
                    pltpu.matmul_push_rhs(w_ref[slot, top:top + HELD, part], staging_register=0, mxu_index=q, transpose=True)
                    pltpu.matmul_acc_lhs(moved[q], w_ref[slot, top + HELD:top + HELD + MOVED, part], load_staged_rhs=1)
                    if not (last and k == depth - 1):
                        hold_x((k + 1) % depth, q)
                    pltpu.matmul_acc_lhs(held[q], n_ref[:, part], load_staged_rhs=0)
            wide_tiles = []
            tiles, hits = [], []
            for q in range(UNITS):
                row = first_row + q * (HELD + MOVED)
                logits = pltpu.matmul_pop(moved[q])
                tiles += tall_tiles(logits)
                hits += tall_hits(row + HELD, MOVED // SUBLANES)
            tall = fold(tall, tiles, hits, None)
            for q in range(UNITS):
                row = first_row + q * (HELD + MOVED)
                logits = pltpu.matmul_pop(held[q])
                for c in range(HELD // LANES):
                    wide_tiles.append((logits[:, c * LANES:(c + 1) * LANES], row + c * LANES))
            for t in range(positions):
                here = slice(t * SUBLANES, (t + 1) * SUBLANES)
                state = tuple(state_ref[s, t] for s in range(4))
                state = fold(state, [z[here] for z, _ in wide_tiles], [wide_ids[t] == row for _, row in wide_tiles], trip == 0)
                for s in range(4):
                    state_ref[s, t] = state[s]
            return tall

        def body(trip, tall):
            slot = lax.rem(trip, SLOTS)
            tall = trip_step(trip, slot, tall, False)
            return tall

        def filling(trip, tall):
            tall = body(trip, tall)
            fetch(trip + SLOTS, lax.rem(trip, SLOTS)).start()
            return tall

        tall = lax.fori_loop(0, trips - 1 - SLOTS, filling, tall)
        tall = body(trips - 1 - SLOTS, tall)
        for c in range(CUTS):
            fetch_cut(c).start()
        tall = lax.fori_loop(trips - SLOTS, trips - 1, body, tall)
        tall = trip_step(trips - 1, (trips - 1) % SLOTS, tall, True)

        row_max, exp_sum, weighted, picked = tall
        top = jnp.max(row_max, axis=0, keepdims=True)
        drop = row_max - top
        scale = jnp.exp(drop)
        tall_row = [jnp.broadcast_to(v, (SUBLANES, LANES)) for v in (
            top, jnp.sum(scale * exp_sum, axis=0, keepdims=True),
            jnp.sum(scale * (weighted + drop * exp_sum), axis=0, keepdims=True), jnp.sum(picked, axis=0, keepdims=True))]
        packed = jnp.zeros((SUBLANES, LANES), jnp.float32)
        for t in range(positions):
            row_max, exp_sum, weighted, picked = (state_ref[s, t] for s in range(4))
            own = lane == t * batch + sub
            top = jnp.max(jnp.where(own, jnp.maximum(row_max, tall_row[0]), row_max), axis=1, keepdims=True)
            drop, far = row_max - top, jnp.where(own, tall_row[0] - top, 0.0)
            scale, other = jnp.exp(drop), jnp.exp(far)
            values = (top,
                      jnp.sum(scale * exp_sum + jnp.where(own, other * tall_row[1], 0.0), axis=1, keepdims=True),
                      jnp.sum(scale * (weighted + drop * exp_sum) + jnp.where(own, other * (tall_row[2] + far * tall_row[1]), 0.0), axis=1, keepdims=True),
                      jnp.sum(picked + jnp.where(own, tall_row[3], 0.0), axis=1, keepdims=True))
            for s, v in enumerate(values):
                packed = jnp.where(lane == s * FIELD + t, v, packed)
        stats_ref[...] = packed

    acc = pltpu.ACC
    f32 = jnp.float32
    pl.run_scoped(main, *[acc(q)((n_ref.shape[0], UNIT), f32) for q in range(UNITS)],
                  *[acc(q)((MOVED, UNIT), f32) for q in range(UNITS)],
                  *[acc(q)((edge // UNITS, UNIT), f32) for q in range(UNITS)])


def exchange(n, mine_ref, all_ref, send_sem, recv_sem):
    me = lax.axis_index('tp')
    group = lax.axis_index('dp')
    barrier = pltpu.get_barrier_semaphore()
    for o in range(1, n):
        pl.semaphore_signal(barrier, inc=1, device_id=(group, lax.rem(me + o, n)), device_id_type=MESH)
    all_ref[me] = mine_ref[...]
    pl.semaphore_wait(barrier, n - 1)
    copies = []
    for o in range(1, n):
        copy = pltpu.make_async_remote_copy(
            src_ref=mine_ref, dst_ref=all_ref.at[me], send_sem=send_sem.at[o], recv_sem=recv_sem.at[o],
            device_id=(group, lax.rem(me + o, n)), device_id_type=MESH)
        copy.start()
        copies.append(copy)
    for copy in copies:
        copy.wait()


def combine(n, all_ref, logp_ref, norm_ref, ent_ref):
    parts = [all_ref[d] for d in range(n)]
    fields = [[p if s == 0 else pltpu.roll(p, LANES - s * FIELD, 1) for p in parts] for s in range(4)]
    top = functools.reduce(jnp.maximum, fields[0])
    exp_sum = weighted = picked = jnp.zeros((SUBLANES, LANES), jnp.float32)
    for d in range(n):
        drop = fields[0][d] - top
        scale = jnp.exp(drop)
        exp_sum = exp_sum + scale * fields[1][d]
        weighted = weighted + scale * (fields[2][d] + drop * fields[1][d])
        picked = picked + fields[3][d]
    log_sum = jnp.log(exp_sum)
    log_norm = top + log_sum
    logp_ref[...] = (picked - log_norm)[:, :logp_ref.shape[1]]
    norm_ref[...] = log_norm[:, :norm_ref.shape[1]]
    ent_ref[...] = (log_sum - weighted / exp_sum)[:, :ent_ref.shape[1]]


def solution(mesh):
    n = mesh.shape['tp']

    def per_device(hidden, draft_ids, norm_gain, head_w):
        batch, positions, dim = hidden.shape
        drafts = draft_ids.shape[1]
        rows = batch * positions
        cols = head_w.shape[1]
        x = hidden.transpose(1, 0, 2).reshape(rows, dim)
        gain = norm_gain.reshape(dim // LANES, LANES)
        vmem = pl.BlockSpec(memory_space=pltpu.VMEM)
        hbm = pl.BlockSpec(memory_space=pltpu.HBM)
        tile = jax.ShapeDtypeStruct((SUBLANES, LANES), jnp.float32)
        mine = pl.pallas_call(
            score,
            out_shape=tile,
            in_specs=[hbm, vmem, vmem, hbm],
            out_specs=vmem,
            scratch_shapes=[
                pltpu.VMEM((rows, dim), jnp.bfloat16),
                pltpu.VMEM((pl.cdiv(rows, PACK) * PACK, dim), jnp.bfloat16),
                pltpu.VMEM((dim, LANES), jnp.bfloat16),
                pltpu.VMEM((SLOTS, TRIP, dim), jnp.bfloat16),
                pltpu.VMEM((cols % TRIP, dim), jnp.bfloat16),
                pltpu.VMEM((4, positions, SUBLANES, LANES), jnp.float32),
                pltpu.SemaphoreType.DMA,
                pltpu.SemaphoreType.DMA((SLOTS,)),
                pltpu.SemaphoreType.DMA,
                pltpu.SemaphoreType.DMA((CUTS,)),
            ],
            compiler_params=pltpu.CompilerParams(vmem_limit_bytes=60 * 1024 * 1024),
        )(x, draft_ids, gain, head_w.T)
        every = pl.pallas_call(
            functools.partial(exchange, n),
            out_shape=jax.ShapeDtypeStruct((n, SUBLANES, LANES), jnp.float32),
            in_specs=[vmem],
            out_specs=vmem,
            scratch_shapes=[pltpu.SemaphoreType.DMA((n,)), pltpu.SemaphoreType.DMA((n,))],
            compiler_params=pltpu.CompilerParams(collective_id=0, has_side_effects=True, vmem_limit_bytes=1024 * 1024),
        )(mine)
        return pl.pallas_call(
            functools.partial(combine, n),
            out_shape=(jax.ShapeDtypeStruct((batch, drafts), jnp.float32),
                       jax.ShapeDtypeStruct((batch, positions), jnp.float32),
                       jax.ShapeDtypeStruct((batch, positions), jnp.float32)),
            in_specs=[vmem],
            out_specs=(vmem, vmem, vmem),
            compiler_params=pltpu.CompilerParams(vmem_limit_bytes=1024 * 1024),
        )(every)

    specs_in = (P('dp', None, None), P('dp', None), P(None), P(None, 'tp'))
    specs_out = (P('dp', None), P('dp', None), P('dp', None))
    return jax.shard_map(per_device, mesh=mesh, in_specs=specs_in, out_specs=specs_out, check_vma=False)
```

time: 291 us -> 51.5 us (0.18)
  waiting for transfers between devices: 174 us -> 0 us
  matrix products: 50.5 us -> 0 us
  Pallas kernels: 0 us -> 50 us
  other arithmetic: 49.3 us -> 0 us
  between operations: 14.1 us -> 0.66 us
    all_gather x1 -> x0, waiting for transfers between devices: 174 us -> none  [per_device(): gathered = lax.all_gather(logits, 'tp')]
    dot_general x1 -> x0, matrix products: 50.5 us -> none  [per_device(): jnp.einsum('btd,dv->btv', normed, head_w, preferred_element_type=jnp.floa...]
    pallas_call x0 -> x3, Pallas kernels: none -> 50 us  [the longest x1 42.6 us: per_device(): pl.pallas_call(score, out_shape=tile, in_specs=[hbm, vmem, vmem, hbm], ou...]
    reduce_sum x3 -> x0, other arithmetic: 34.9 us -> none  [the longest x1 20.5 us: per_device(): weighted = jnp.sum(exp_vals * shifted, axis=(0, 3))]
    reduce_max x2 -> x0, other arithmetic: 13.5 us -> none  [per_device(): row_max = jnp.max(gathered, axis=(0, 3))]
  transfers between devices with their start and end apart: 1 -> 0, of which waited for: 1 -> 0; matrix products, arithmetic and copies ran while one was open for 0% -> 0% of each run, Pallas kernels for 0% -> 0%
where the time goes in v2:
time: 51.5 us; the launch traced here: 51.3 us
  Pallas kernels  50 us (97%)
  local copies, waits for them, and re-layouts  0.68 us (1%)
  between operations  0.66 us (1%)
    pallas_call x1, Pallas kernels, per_device(): pl.pallas_call(score, out_shape=tile, in_specs=[hbm, vmem, vmem, hbm], ou...  42.6 us
    pallas_call x1, Pallas kernels, per_device(): pl.pallas_call(functools.partial(exchange, n), out_shape=jax.ShapeDtypeSt...  6.7 us

profile of v2, /device:TPU:0, one launch (start us, length us, event | category | flops | bytes accessed | tf_op | source)
XLA Modules:
  0.0 51.3 jit_solution(10227822465791280104)
XLA Ops:
  0.6 42.6 %shard_map.67.mine_ref = f32[8,128]{1,0:T(8,128)} custom-call(bf16[72,4096]{1,0:T(8,128)(2,1)} %bitcast.5, s32[8,8]{1,0:T(8,128)} %ids_ref.1, bf16[32,128]{1,0:T(8,128)(2,1)} %bitcast.6, bf16[16032,4096]{1,0:T(8,128)(2,1)} %bitcast.3.w_hbm), custom_call_target="tpu_custom_call" | custom-call | tf_op jit(solution)/shard_map/pallas_call | solution.py:257
  43.2 0.0 copy-start
  43.2 0.7 %copy-done = f32[8,128]{1,0:T(8,128)S(1)} copy-done((f32[8,128]{1,0:T(8,128)S(1)}, f32[8,128]{1,0:T(8,128)}, u32[]{:S(2)}) %copy-start) | copy-done | bytes 4120
  43.9 6.7 %shard_map.68.all_ref = f32[8,8,128]{2,1,0:T(8,128)S(1)} custom-call(f32[8,128]{1,0:T(8,128)S(1)} %copy-done), custom_call_target="tpu_custom_call" | custom-call | tf_op jit(solution)/shard_map/pallas_call | solution.py:276
  50.6 0.7 %shard_map.69 = (f32[8,8]{1,0:T(8,128)}, f32[8,9]{1,0:T(8,128)}, f32[8,9]{1,0:T(8,128)}) custom-call(f32[8,8,128]{2,1,0:T(8,128)S(1)} %shard_map.68.all_ref), custom_call_target="tpu_custom_call" | custom-call | tf_op jit(solution)/shard_map/pallas_call | solution.py:284
Async XLA Ops:
  43.2 0.7 %copy-start = (f32[8,128]{1,0:T(8,128)S(1)}, f32[8,128]{1,0:T(8,128)}, u32[]{:S(2)}) copy-start(f32[8,128]{1,0:T(8,128)} %shard_map.67.mine_ref) | copy-start | bytes 12292

commit v3 on v2

--- a/solution.py
+++ b/solution.py
@@ -17,8 +17,9 @@
 MOVED = 304
 UNITS = 2
 TRIP = UNITS * (HELD + MOVED)
-SLOTS = 5
-CUTS = 4
+SLOTS = 4
+CUTS = 8
+SCORE_VMEM = 46 * 1024 * 1024
 FIELD = 16
 
 
@@ -39,8 +40,16 @@
     return new_max, exp_sum, weighted, picked
 
 
-def score(x_hbm, ids_ref, gain_ref, w_hbm, stats_ref,
-          x_ref, n_ref, xt_ref, w_ref, edge_ref, state_ref, x_sem, w_sem, edge_sem, cut_sem):
+def tall_tiles(logits):
+    return [logits[r:r + SUBLANES, :LANES] for r in range(0, logits.shape[0], SUBLANES)]
+
+
+def tall_hits(tall_ids, first_row, count):
+    return [(tall_ids - first_row) == r * SUBLANES for r in range(count)]
+
+
+def score(x_hbm, ids_hbm, gain_hbm, w_hbm, tall_ref, state_ref, ids_out, moved_ref, held_ref,
+          x_ref, ids_ref, gain_ref, n_ref, xt_ref, w_ref, edge_ref, in_sem, w_sem, edge_sem, cut_sem):
     me = lax.axis_index('tp')
     batch, drafts = ids_ref.shape
     rows = x_hbm.shape[0]
@@ -59,8 +68,10 @@
         part = pl.ds(c * cut, cut)
         return pltpu.make_async_copy(w_hbm.at[pl.ds(cols - TRIP, TRIP), part], w_ref.at[(trips - 1) % SLOTS, :, part], cut_sem.at[c])
 
-    x_copy = pltpu.make_async_copy(x_hbm, x_ref, x_sem)
-    x_copy.start()
+    inputs = [pltpu.make_async_copy(src, dst, in_sem.at[i])
+              for i, (src, dst) in enumerate(((x_hbm, x_ref), (ids_hbm, ids_ref), (gain_hbm, gain_ref)))]
+    for copy in inputs:
+        copy.start()
     edge_copy = pltpu.make_async_copy(w_hbm.at[pl.ds(0, edge)], edge_ref, edge_sem)
     edge_copy.start()
     for b in range(SLOTS):
@@ -68,6 +79,8 @@
 
     lane = lax.broadcasted_iota(jnp.int32, (SUBLANES, LANES), 1)
     sub = lax.broadcasted_iota(jnp.int32, (SUBLANES, LANES), 0)
+    for copy in inputs:
+        copy.wait()
     ids = ids_ref[...] - me * cols
     nobody = jnp.full((SUBLANES, LANES), -(1 << 29), jnp.int32)
     wide_ids = [ids[:, t:t + 1] - lane for t in range(drafts)] + [nobody] * (positions - drafts)
@@ -76,7 +89,6 @@
         spread = jnp.sum(jnp.where(lane == t * batch + sub, ids[:, t:t + 1], 0), axis=0, keepdims=True)
         tall_ids = jnp.where(lane // batch == t, spread - sub, tall_ids)
 
-    x_copy.wait()
     total = jnp.zeros((rows, LANES), jnp.float32)
     for c in range(dim // LANES):
         wide = x_ref[:, c * LANES:(c + 1) * LANES].astype(jnp.float32)
@@ -95,11 +107,9 @@
     def hold_x(k, q):
         pltpu.matmul_push_rhs(jnp.concatenate([xt_ref[k * UNIT:(k + 1) * UNIT, :], zeros], axis=1), staging_register=1, mxu_index=q)
 
-    def tall_tiles(logits):
-        return [logits[r:r + SUBLANES, :LANES] for r in range(0, logits.shape[0], SUBLANES)]
-
-    def tall_hits(first_row, count):
-        return [(tall_ids - first_row) == r * SUBLANES for r in range(count)]
+    for t in range(positions):
+        ids_out[t] = wide_ids[t]
+    ids_out[positions] = tall_ids
 
     def main(held_0, held_1, moved_0, moved_1, edge_0, edge_1):
         held, moved, edges = (held_0, held_1), (moved_0, moved_1), (edge_0, edge_1)
@@ -117,7 +127,7 @@
         tiles, hits = [], []
         for q in range(UNITS):
             tiles += tall_tiles(pltpu.matmul_pop(edges[q]))
-            hits += tall_hits(q * half, half // SUBLANES)
+            hits += tall_hits(tall_ids, q * half, half // SUBLANES)
         zero = jnp.zeros((SUBLANES, LANES), jnp.float32)
         tall = fold((tiles[0], zero, zero, zero), tiles, hits, None)
         state_ref[...] = jnp.zeros_like(state_ref)
@@ -137,13 +147,19 @@
                     if not (last and k == depth - 1):
                         hold_x((k + 1) % depth, q)
                     pltpu.matmul_acc_lhs(held[q], n_ref[:, part], load_staged_rhs=0)
+            if last:
+                for q in range(UNITS):
+                    moved_ref[q] = pltpu.matmul_pop(moved[q])[:, :LANES]
+                for q in range(UNITS):
+                    held_ref[q] = pltpu.matmul_pop(held[q])
+                return tall
             wide_tiles = []
             tiles, hits = [], []
             for q in range(UNITS):
                 row = first_row + q * (HELD + MOVED)
                 logits = pltpu.matmul_pop(moved[q])
                 tiles += tall_tiles(logits)
-                hits += tall_hits(row + HELD, MOVED // SUBLANES)
+                hits += tall_hits(tall_ids, row + HELD, MOVED // SUBLANES)
             tall = fold(tall, tiles, hits, None)
             for q in range(UNITS):
                 row = first_row + q * (HELD + MOVED)
@@ -175,27 +191,8 @@
         tall = lax.fori_loop(trips - SLOTS, trips - 1, body, tall)
         tall = trip_step(trips - 1, (trips - 1) % SLOTS, tall, True)
 
-        row_max, exp_sum, weighted, picked = tall
-        top = jnp.max(row_max, axis=0, keepdims=True)
-        drop = row_max - top
-        scale = jnp.exp(drop)
-        tall_row = [jnp.broadcast_to(v, (SUBLANES, LANES)) for v in (
-            top, jnp.sum(scale * exp_sum, axis=0, keepdims=True),
-            jnp.sum(scale * (weighted + drop * exp_sum), axis=0, keepdims=True), jnp.sum(picked, axis=0, keepdims=True))]
-        packed = jnp.zeros((SUBLANES, LANES), jnp.float32)
-        for t in range(positions):
-            row_max, exp_sum, weighted, picked = (state_ref[s, t] for s in range(4))
-            own = lane == t * batch + sub
-            top = jnp.max(jnp.where(own, jnp.maximum(row_max, tall_row[0]), row_max), axis=1, keepdims=True)
-            drop, far = row_max - top, jnp.where(own, tall_row[0] - top, 0.0)
-            scale, other = jnp.exp(drop), jnp.exp(far)
-            values = (top,
-                      jnp.sum(scale * exp_sum + jnp.where(own, other * tall_row[1], 0.0), axis=1, keepdims=True),
-                      jnp.sum(scale * (weighted + drop * exp_sum) + jnp.where(own, other * (tall_row[2] + far * tall_row[1]), 0.0), axis=1, keepdims=True),
-                      jnp.sum(picked + jnp.where(own, tall_row[3], 0.0), axis=1, keepdims=True))
-            for s, v in enumerate(values):
-                packed = jnp.where(lane == s * FIELD + t, v, packed)
-        stats_ref[...] = packed
+        for s in range(4):
+            tall_ref[s] = tall[s]
 
     acc = pltpu.ACC
     f32 = jnp.float32
@@ -204,19 +201,62 @@
                   *[acc(q)((edge // UNITS, UNIT), f32) for q in range(UNITS)])
 
 
-def exchange(n, mine_ref, all_ref, send_sem, recv_sem):
+def exchange(n, last_row, tall_ref, state_ref, ids_ref, moved_ref, held_ref, all_ref, mine_ref, send_sem, recv_sem):
     me = lax.axis_index('tp')
     group = lax.axis_index('dp')
+    batch, positions = SUBLANES, state_ref.shape[1]
+    bits = [(d, lax.rem(me // d, 2)) for d in (1, 2, 4)]
+    order = [o for o in (6, 7, 4, 5, 2, 3, 1) if o < n]
+    peers = {o: me + sum(d * (1 - 2 * b) for d, b in bits if o & d) for o in order}
     barrier = pltpu.get_barrier_semaphore()
-    for o in range(1, n):
-        pl.semaphore_signal(barrier, inc=1, device_id=(group, lax.rem(me + o, n)), device_id_type=MESH)
-    all_ref[me] = mine_ref[...]
+    for o in order:
+        pl.semaphore_signal(barrier, inc=1, device_id=(group, peers[o]), device_id_type=MESH)
+
+    lane = lax.broadcasted_iota(jnp.int32, (SUBLANES, LANES), 1)
+    sub = lax.broadcasted_iota(jnp.int32, (SUBLANES, LANES), 0)
+    tiles, hits = [], []
+    for q in range(UNITS):
+        row = last_row + q * (HELD + MOVED)
+        tiles += tall_tiles(moved_ref[q])
+        hits += tall_hits(ids_ref[positions], row + HELD, MOVED // SUBLANES)
+    tall = fold(tuple(tall_ref[s] for s in range(4)), tiles, hits, None)
+    wide = []
+    for t in range(positions):
+        tiles, hits = [], []
+        for q in range(UNITS):
+            for c in range(HELD // LANES):
+                tiles.append(held_ref[q, t * SUBLANES:(t + 1) * SUBLANES, c * LANES:(c + 1) * LANES])
+                hits.append(ids_ref[t] == last_row + q * (HELD + MOVED) + c * LANES)
+        wide.append(fold(tuple(state_ref[s, t] for s in range(4)), tiles, hits, None))
+
+    row_max, exp_sum, weighted, picked = tall
+    top = jnp.max(row_max, axis=0, keepdims=True)
+    drop = row_max - top
+    scale = jnp.exp(drop)
+    flat = [jnp.broadcast_to(v, (SUBLANES, LANES)) for v in (
+        top, jnp.sum(scale * exp_sum, axis=0, keepdims=True),
+        jnp.sum(scale * (weighted + drop * exp_sum), axis=0, keepdims=True), jnp.sum(picked, axis=0, keepdims=True))]
+    packed = jnp.zeros((SUBLANES, LANES), jnp.float32)
+    for t in range(positions):
+        row_max, exp_sum, weighted, picked = wide[t]
+        own = lane == t * batch + sub
+        top = jnp.max(jnp.where(own, jnp.maximum(row_max, flat[0]), row_max), axis=1, keepdims=True)
+        drop, far = row_max - top, jnp.where(own, flat[0] - top, 0.0)
+        scale, other = jnp.exp(drop), jnp.exp(far)
+        values = (top,
+                  jnp.sum(scale * exp_sum + jnp.where(own, other * flat[1], 0.0), axis=1, keepdims=True),
+                  jnp.sum(scale * (weighted + drop * exp_sum) + jnp.where(own, other * (flat[2] + far * flat[1]), 0.0), axis=1, keepdims=True),
+                  jnp.sum(picked + jnp.where(own, flat[3], 0.0), axis=1, keepdims=True))
+        for s, v in enumerate(values):
+            packed = jnp.where(lane == s * FIELD + t, v, packed)
+    mine_ref[...] = packed
+    all_ref[me] = packed
     pl.semaphore_wait(barrier, n - 1)
     copies = []
-    for o in range(1, n):
+    for o in order:
         copy = pltpu.make_async_remote_copy(
             src_ref=mine_ref, dst_ref=all_ref.at[me], send_sem=send_sem.at[o], recv_sem=recv_sem.at[o],
-            device_id=(group, lax.rem(me + o, n)), device_id_type=MESH)
+            device_id=(group, peers[o]), device_id_type=MESH)
         copy.start()
         copies.append(copy)
     for copy in copies:
@@ -253,34 +293,40 @@
         gain = norm_gain.reshape(dim // LANES, LANES)
         vmem = pl.BlockSpec(memory_space=pltpu.VMEM)
         hbm = pl.BlockSpec(memory_space=pltpu.HBM)
-        tile = jax.ShapeDtypeStruct((SUBLANES, LANES), jnp.float32)
-        mine = pl.pallas_call(
+        f32 = jnp.float32
+        padded = pl.cdiv(rows, PACK) * PACK
+        partial = pl.pallas_call(
             score,
-            out_shape=tile,
-            in_specs=[hbm, vmem, vmem, hbm],
-            out_specs=vmem,
+            out_shape=(jax.ShapeDtypeStruct((4, SUBLANES, LANES), f32),
+                       jax.ShapeDtypeStruct((4, positions, SUBLANES, LANES), f32),
+                       jax.ShapeDtypeStruct((positions + 1, SUBLANES, LANES), jnp.int32),
+                       jax.ShapeDtypeStruct((UNITS, MOVED, LANES), f32),
+                       jax.ShapeDtypeStruct((UNITS, padded, UNIT), f32)),
+            in_specs=[hbm] * 4,
+            out_specs=(vmem,) * 5,
             scratch_shapes=[
                 pltpu.VMEM((rows, dim), jnp.bfloat16),
-                pltpu.VMEM((pl.cdiv(rows, PACK) * PACK, dim), jnp.bfloat16),
+                pltpu.VMEM((batch, drafts), jnp.int32),
+                pltpu.VMEM((dim // LANES, LANES), jnp.bfloat16),
+                pltpu.VMEM((padded, dim), jnp.bfloat16),
                 pltpu.VMEM((dim, LANES), jnp.bfloat16),
                 pltpu.VMEM((SLOTS, TRIP, dim), jnp.bfloat16),
                 pltpu.VMEM((cols % TRIP, dim), jnp.bfloat16),
-                pltpu.VMEM((4, positions, SUBLANES, LANES), jnp.float32),
-                pltpu.SemaphoreType.DMA,
+                pltpu.SemaphoreType.DMA((3,)),
                 pltpu.SemaphoreType.DMA((SLOTS,)),
                 pltpu.SemaphoreType.DMA,
                 pltpu.SemaphoreType.DMA((CUTS,)),
             ],
-            compiler_params=pltpu.CompilerParams(vmem_limit_bytes=60 * 1024 * 1024),
-        )(x, draft_ids, gain, head_w.T)
+            compiler_params=pltpu.CompilerParams(vmem_limit_bytes=SCORE_VMEM),
+        )(*[pltpu.with_memory_space_constraint(v, pltpu.HBM) for v in (x, draft_ids, gain, head_w.T)])
         every = pl.pallas_call(
-            functools.partial(exchange, n),
-            out_shape=jax.ShapeDtypeStruct((n, SUBLANES, LANES), jnp.float32),
-            in_specs=[vmem],
+            functools.partial(exchange, n, cols - TRIP),
+            out_shape=jax.ShapeDtypeStruct((n, SUBLANES, LANES), f32),
+            in_specs=[vmem] * 5,
             out_specs=vmem,
-            scratch_shapes=[pltpu.SemaphoreType.DMA((n,)), pltpu.SemaphoreType.DMA((n,))],
-            compiler_params=pltpu.CompilerParams(collective_id=0, has_side_effects=True, vmem_limit_bytes=1024 * 1024),
-        )(mine)
+            scratch_shapes=[pltpu.VMEM((SUBLANES, LANES), f32), pltpu.SemaphoreType.DMA((n,)), pltpu.SemaphoreType.DMA((n,))],
+            compiler_params=pltpu.CompilerParams(collective_id=0, has_side_effects=True, vmem_limit_bytes=4 * 1024 * 1024),
+        )(*partial)
         return pl.pallas_call(
             functools.partial(combine, n),
             out_shape=(jax.ShapeDtypeStruct((batch, drafts), jnp.float32),

time: 51.5 us -> 49.5 us (0.961)
  Pallas kernels: 50 us -> 48.8 us
  local copies, waits for them, and re-layouts: 0.68 us -> 0 us
    pallas_call x2, Pallas kernels: 49.3 us -> 48.1 us  [the longest x1 41.4 us: per_device(): pl.pallas_call(score, out_shape=(jax.ShapeDtypeStruct((4, SUBLANES, LANES...]
    unnamed x2 -> x0, local copies, waits for them, and re-layouts: 0.68 us -> none
where the time goes in v3:
time: 49.5 us; the launch traced here: 49.4 us
  Pallas kernels  48.8 us (99%)
  between operations  0.65 us (1%)
    pallas_call x1, Pallas kernels, per_device(): pl.pallas_call(score, out_shape=(jax.ShapeDtypeStruct((4, SUBLANES, LANES...  41.4 us
    pallas_call x1, Pallas kernels, per_device(): pl.pallas_call(functools.partial(exchange, n, cols - TRIP), out_shape=jax...  6.7 us

profile of v3, /device:TPU:0, one launch (start us, length us, event | category | flops | bytes accessed | tf_op | source)
XLA Modules:
  0.0 49.4 jit_solution(8352114214067699201)
XLA Ops:
  0.6 41.4 %shard_map.67 = (f32[4,8,128]{2,1,0:T(8,128)S(1)}, f32[4,9,8,128]{3,2,1,0:T(8,128)S(1)}, s32[10,8,128]{2,1,0:T(8,128)S(1)}, f32[2,304,128]{2,1,0:T(8,128)S(1)}, f32[2,80,256]{2,1,0:T(8,128)S(1)}) custom-call(bf16[72,4096]{1,0:T(8,128)(2,1)} %bitcast.5, s32[8,8]{1,0:T(8,128)} %ids_hbm.1, bf16[32,128]{1,0:T(8,128)(2,1)} %bitcast.6, ...), custom_call_target="tpu_custom_call" | custom-call | tf_op jit(solution)/shard_map/pallas_call | solution.py:298
  42.0 6.7 %shard_map.68.all_ref = f32[8,8,128]{2,1,0:T(8,128)S(1)} custom-call(f32[4,8,128]{2,1,0:T(8,128)S(1)} %get-tuple-element.8.tall_ref, f32[4,9,8,128]{3,2,1,0:T(8,128)S(1)} %get-tuple-element.9.state_ref, s32[10,8,128]{2,1,0:T(8,128)S(1)} %get-tuple-element.10.ids_ref, f32[2,304,128]{2,1,0:T(8,128)S(1)} %get-tuple-element.11.moved_ref, ...), custom_call_target="tpu_custom_call" | custom-call | tf_op jit(solution)/shard_map/pallas_call | solution.py:322
  48.7 0.7 %shard_map.69 = (f32[8,8]{1,0:T(8,128)}, f32[8,9]{1,0:T(8,128)}, f32[8,9]{1,0:T(8,128)}) custom-call(f32[8,8,128]{2,1,0:T(8,128)S(1)} %shard_map.68.all_ref), custom_call_target="tpu_custom_call" | custom-call | tf_op jit(solution)/shard_map/pallas_call | solution.py:330

commit v4 on v3

--- a/solution.py
+++ b/solution.py
@@ -18,7 +18,8 @@
 UNITS = 2
 TRIP = UNITS * (HELD + MOVED)
 SLOTS = 4
-CUTS = 8
+CUTS = 2
+LATE_CUTS = (4, 8)
 SCORE_VMEM = 46 * 1024 * 1024
 FIELD = 16
 
@@ -49,7 +50,7 @@
 
 
 def score(x_hbm, ids_hbm, gain_hbm, w_hbm, tall_ref, state_ref, ids_out, moved_ref, held_ref,
-          x_ref, ids_ref, gain_ref, n_ref, xt_ref, w_ref, edge_ref, in_sem, w_sem, edge_sem, cut_sem):
+          x_ref, ids_ref, gain_ref, n_ref, xt_ref, w_ref, edge_ref, in_sem, w_sem, edge_sem):
     me = lax.axis_index('tp')
     batch, drafts = ids_ref.shape
     rows = x_hbm.shape[0]
@@ -58,15 +59,16 @@
     depth = dim // UNIT
     trips = cols // TRIP
     edge = cols - trips * TRIP
-    cut = dim // CUTS
-
-    def fetch(trip, slot):
+    late = trips - len(LATE_CUTS)
+
+    def fetch(trip, slot, cuts, c):
         start = pl.multiple_of(edge + trip * TRIP, SUBLANES)
-        return pltpu.make_async_copy(w_hbm.at[pl.ds(start, TRIP)], w_ref.at[slot], w_sem.at[slot])
-
-    def fetch_cut(c):
-        part = pl.ds(c * cut, cut)
-        return pltpu.make_async_copy(w_hbm.at[pl.ds(cols - TRIP, TRIP), part], w_ref.at[(trips - 1) % SLOTS, :, part], cut_sem.at[c])
+        part = pl.ds(c * (dim // cuts), dim // cuts)
+        return pltpu.make_async_copy(w_hbm.at[pl.ds(start, TRIP), part], w_ref.at[slot, :, part], w_sem.at[slot, c])
+
+    def begin(trip, slot, cuts=CUTS):
+        for c in range(cuts):
+            fetch(trip, slot, cuts, c).start(priority=1)
 
     inputs = [pltpu.make_async_copy(src, dst, in_sem.at[i])
               for i, (src, dst) in enumerate(((x_hbm, x_ref), (ids_hbm, ids_ref), (gain_hbm, gain_ref)))]
@@ -75,7 +77,7 @@
     edge_copy = pltpu.make_async_copy(w_hbm.at[pl.ds(0, edge)], edge_ref, edge_sem)
     edge_copy.start()
     for b in range(SLOTS):
-        fetch(b, b).start()
+        begin(b, b)
 
     lane = lax.broadcasted_iota(jnp.int32, (SUBLANES, LANES), 1)
     sub = lax.broadcasted_iota(jnp.int32, (SUBLANES, LANES), 0)
@@ -132,13 +134,11 @@
         tall = fold((tiles[0], zero, zero, zero), tiles, hits, None)
         state_ref[...] = jnp.zeros_like(state_ref)
 
-        def trip_step(trip, slot, tall, last):
-            if not last:
-                fetch(trip, slot).wait()
+        def trip_step(trip, slot, tall, cuts=CUTS, last=False):
             first_row = edge + trip * TRIP
             for k in range(depth):
-                if last and k % (depth // CUTS) == 0:
-                    fetch_cut(k // (depth // CUTS)).wait()
+                if k % (depth // cuts) == 0:
+                    fetch(trip, slot, cuts, k // (depth // cuts)).wait()
                 part = slice(k * UNIT, (k + 1) * UNIT)
                 for q in range(UNITS):
                     top = q * (HELD + MOVED)
@@ -176,20 +176,23 @@
 
         def body(trip, tall):
             slot = lax.rem(trip, SLOTS)
-            tall = trip_step(trip, slot, tall, False)
+            tall = trip_step(trip, slot, tall)
+            ahead = trip + SLOTS
+
+            @pl.when(ahead < late)
+            def _():
+                begin(ahead, slot)
+
+            for i, cuts in enumerate(LATE_CUTS):
+                @pl.when(ahead == late + i)
+                def _():
+                    begin(late + i, (late + i) % SLOTS, cuts)
             return tall
 
-        def filling(trip, tall):
-            tall = body(trip, tall)
-            fetch(trip + SLOTS, lax.rem(trip, SLOTS)).start()
-            return tall
-
-        tall = lax.fori_loop(0, trips - 1 - SLOTS, filling, tall)
-        tall = body(trips - 1 - SLOTS, tall)
-        for c in range(CUTS):
-            fetch_cut(c).start()
-        tall = lax.fori_loop(trips - SLOTS, trips - 1, body, tall)
-        tall = trip_step(trips - 1, (trips - 1) % SLOTS, tall, True)
+        tall = lax.fori_loop(0, late, body, tall)
+        for i, cuts in enumerate(LATE_CUTS):
+            trip = late + i
+            tall = trip_step(trip, trip % SLOTS, tall, cuts, trip == trips - 1)
 
         for s in range(4):
             tall_ref[s] = tall[s]
@@ -313,9 +316,8 @@
                 pltpu.VMEM((SLOTS, TRIP, dim), jnp.bfloat16),
                 pltpu.VMEM((cols % TRIP, dim), jnp.bfloat16),
                 pltpu.SemaphoreType.DMA((3,)),
-                pltpu.SemaphoreType.DMA((SLOTS,)),
+                pltpu.SemaphoreType.DMA((SLOTS, max(CUTS, *LATE_CUTS))),
                 pltpu.SemaphoreType.DMA,
-                pltpu.SemaphoreType.DMA((CUTS,)),
             ],
             compiler_params=pltpu.CompilerParams(vmem_limit_bytes=SCORE_VMEM),
         )(*[pltpu.with_memory_space_constraint(v, pltpu.HBM) for v in (x, draft_ids, gain, head_w.T)])

time: 49.5 us -> 47.8 us (0.966)
  Pallas kernels: 48.8 us -> 47.1 us
    pallas_call x1, Pallas kernels: 41.4 us -> 39.7 us  [per_device(): pl.pallas_call(score, out_shape=(jax.ShapeDtypeStruct((4, SUBLANES, LANES...]
where the time goes in v4:
time: 47.8 us; the launch traced here: 47.7 us
  Pallas kernels  47.1 us (99%)
  between operations  0.65 us (1%)
    pallas_call x1, Pallas kernels, per_device(): pl.pallas_call(score, out_shape=(jax.ShapeDtypeStruct((4, SUBLANES, LANES...  39.7 us
    pallas_call x1, Pallas kernels, per_device(): pl.pallas_call(functools.partial(exchange, n, cols - TRIP), out_shape=jax...  6.71 us

profile of v4, /device:TPU:0, one launch (start us, length us, event | category | flops | bytes accessed | tf_op | source)
XLA Modules:
  0.0 47.7 jit_solution(4933317509628453051)
XLA Ops:
  0.6 39.7 %shard_map.67 = (f32[4,8,128]{2,1,0:T(8,128)S(1)}, f32[4,9,8,128]{3,2,1,0:T(8,128)S(1)}, s32[10,8,128]{2,1,0:T(8,128)S(1)}, f32[2,304,128]{2,1,0:T(8,128)S(1)}, f32[2,80,256]{2,1,0:T(8,128)S(1)}) custom-call(bf16[72,4096]{1,0:T(8,128)(2,1)} %bitcast.5, s32[8,8]{1,0:T(8,128)} %ids_hbm.1, bf16[32,128]{1,0:T(8,128)(2,1)} %bitcast.6, ...), custom_call_target="tpu_custom_call" | custom-call | tf_op jit(solution)/shard_map/pallas_call | solution.py:301
  40.3 6.7 %shard_map.68.all_ref = f32[8,8,128]{2,1,0:T(8,128)S(1)} custom-call(f32[4,8,128]{2,1,0:T(8,128)S(1)} %get-tuple-element.8.tall_ref, f32[4,9,8,128]{3,2,1,0:T(8,128)S(1)} %get-tuple-element.9.state_ref, s32[10,8,128]{2,1,0:T(8,128)S(1)} %get-tuple-element.10.ids_ref, f32[2,304,128]{2,1,0:T(8,128)S(1)} %get-tuple-element.11.moved_ref, ...), custom_call_target="tpu_custom_call" | custom-call | tf_op jit(solution)/shard_map/pallas_call | solution.py:324
  47.1 0.7 %shard_map.69 = (f32[8,8]{1,0:T(8,128)}, f32[8,9]{1,0:T(8,128)}, f32[8,9]{1,0:T(8,128)}) custom-call(f32[8,8,128]{2,1,0:T(8,128)S(1)} %shard_map.68.all_ref), custom_call_target="tpu_custom_call" | custom-call | tf_op jit(solution)/shard_map/pallas_call | solution.py:332

commit v5 on v4

v5 whole, which is shorter than its diff:
```python
import functools

import jax
import jax.numpy as jnp
from jax import lax
from jax.experimental import pallas as pl
from jax.experimental.pallas import tpu as pltpu
from jax.sharding import PartitionSpec as P

NORM_EPS = 1e-5
MESH = pl.DeviceIdType.MESH
LANES = 128
SUBLANES = 8
UNIT = 256
PACK = 16
HELD = 256
MOVED = 304
UNITS = 2
TRIP = UNITS * (HELD + MOVED)
SLOTS = 4
CUTS = 2
LATE_CUTS = (4, 4)
SCORE_VMEM = 46 * 1024 * 1024
FIELD = 16


def fold(state, tiles, hits, start):
    row_max, exp_sum, weighted, picked = state
    base = row_max if start is None else jnp.where(start, tiles[0], row_max)
    new_max = functools.reduce(jnp.maximum, tiles, base)
    drop = base - new_max
    scale = jnp.exp(drop)
    weighted = scale * (weighted + drop * exp_sum)
    exp_sum = scale * exp_sum
    for tile, hit in zip(tiles, hits):
        shifted = tile - new_max
        exp_vals = jnp.exp(shifted)
        exp_sum = exp_sum + exp_vals
        weighted = weighted + exp_vals * shifted
        picked = picked + jnp.where(hit, tile, 0.0)
    return new_max, exp_sum, weighted, picked


def tall_tiles(logits):
    return [logits[r:r + SUBLANES, :LANES] for r in range(0, logits.shape[0], SUBLANES)]


def tall_hits(tall_ids, first_row, count):
    return [(tall_ids - first_row) == r * SUBLANES for r in range(count)]


def contract(rows, columns):
    return lax.dot_general(rows, columns, (((1,), (1,)), ((), ())), preferred_element_type=jnp.float32)


def score(n, x_hbm, ids_hbm, gain_hbm, w_hbm, all_ref,
          x_ref, ids_ref, gain_ref, n_ref, xt_ref, w_ref, edge_ref, state_ref, mine_ref,
          in_sem, w_sem, edge_sem, send_sem, recv_sem):
    me = lax.axis_index('tp')
    group = lax.axis_index('dp')
    batch, drafts = ids_ref.shape
    rows = x_hbm.shape[0]
    positions = rows // batch
    cols, dim = w_hbm.shape
    depth = dim // UNIT
    trips = cols // TRIP
    edge = cols - trips * TRIP
    late = trips - len(LATE_CUTS)

    def fetch(trip, slot, cuts, c):
        start = pl.multiple_of(edge + trip * TRIP, SUBLANES)
        part = pl.ds(c * (dim // cuts), dim // cuts)
        return pltpu.make_async_copy(w_hbm.at[pl.ds(start, TRIP), part], w_ref.at[slot, :, part], w_sem.at[slot, c])

    def begin(trip, slot, cuts=CUTS):
        for c in range(cuts):
            fetch(trip, slot, cuts, c).start(priority=1)

    inputs = [pltpu.make_async_copy(src, dst, in_sem.at[i])
              for i, (src, dst) in enumerate(((x_hbm, x_ref), (ids_hbm, ids_ref), (gain_hbm, gain_ref)))]
    for copy in inputs:
        copy.start()
    edge_copy = pltpu.make_async_copy(w_hbm.at[pl.ds(0, edge)], edge_ref, edge_sem)
    edge_copy.start()
    for b in range(SLOTS):
        begin(b, b)

    bits = [(d, lax.rem(me // d, 2)) for d in (1, 2, 4)]
    order = [o for o in (6, 7, 4, 5, 2, 3, 1) if o < n]
    peers = {o: me + sum(d * (1 - 2 * b) for d, b in bits if o & d) for o in order}
    barrier = pltpu.get_barrier_semaphore()
    for o in order:
        pl.semaphore_signal(barrier, inc=1, device_id=(group, peers[o]), device_id_type=MESH)

    for copy in inputs:
        copy.wait()
    lane = lax.broadcasted_iota(jnp.int32, (SUBLANES, LANES), 1)
    sub = lax.broadcasted_iota(jnp.int32, (SUBLANES, LANES), 0)
    ids = ids_ref[...] - me * cols
    nobody = jnp.full((SUBLANES, LANES), -(1 << 29), jnp.int32)
    wide_ids = [ids[:, t:t + 1] - lane for t in range(drafts)] + [nobody] * (positions - drafts)
    tall_ids = nobody
    for t in range(drafts):
        spread = jnp.sum(jnp.where(lane == t * batch + sub, ids[:, t:t + 1], 0), axis=0, keepdims=True)
        tall_ids = jnp.where(lane // batch == t, spread - sub, tall_ids)

    total = jnp.zeros((rows, LANES), jnp.float32)
    for c in range(dim // LANES):
        wide = x_ref[:, c * LANES:(c + 1) * LANES].astype(jnp.float32)
        total = total + wide * wide
    inv_rms = lax.rsqrt(jnp.sum(total, axis=1, keepdims=True) / dim + NORM_EPS)
    gain = gain_ref[...].astype(jnp.float32)
    pad = jnp.zeros((LANES - rows, LANES), jnp.float32)
    for c in range(dim // LANES):
        wide = x_ref[:, c * LANES:(c + 1) * LANES].astype(jnp.float32)
        normed = jnp.concatenate([wide * inv_rms * gain[c:c + 1, :], pad], axis=0)
        n_ref[:, c * LANES:(c + 1) * LANES] = normed[:n_ref.shape[0]].astype(jnp.bfloat16)
        xt_ref[c * LANES:(c + 1) * LANES, :] = normed.T.astype(jnp.bfloat16)
    state_ref[...] = jnp.zeros_like(state_ref)

    def trip_step(trip, slot, tall, cuts=CUTS):
        moved, held = [0.0] * UNITS, [0.0] * UNITS
        for k in range(depth):
            if k % (depth // cuts) == 0:
                fetch(trip, slot, cuts, k // (depth // cuts)).wait()
            part = slice(k * UNIT, (k + 1) * UNIT)
            for q in range(UNITS):
                top = q * (HELD + MOVED)
                moved[q] += jnp.dot(w_ref[slot, top + HELD:top + HELD + MOVED, part], xt_ref[part, :], preferred_element_type=jnp.float32)
                held[q] += contract(n_ref[:, part], w_ref[slot, top:top + HELD, part])
        tiles, hits, wide = [], [], []
        for q in range(UNITS):
            row = edge + trip * TRIP + q * (HELD + MOVED)
            tiles += tall_tiles(moved[q])
            hits += tall_hits(tall_ids, row + HELD, MOVED // SUBLANES)
            wide += [(held[q][:, c:c + LANES], row + c) for c in range(0, HELD, LANES)]
        tall = fold(tall, tiles, hits, None)
        for t in range(positions):
            here = slice(t * SUBLANES, (t + 1) * SUBLANES)
            state = tuple(state_ref[s, t] for s in range(4))
            state = fold(state, [z[here] for z, _ in wide], [wide_ids[t] == row for _, row in wide], trip == 0)
            for s in range(4):
                state_ref[s, t] = state[s]
        return tall

    def body(trip, tall):
        slot = lax.rem(trip, SLOTS)
        tall = trip_step(trip, slot, tall)
        ahead = trip + SLOTS

        @pl.when(ahead < late)
        def _():
            begin(ahead, slot)

        for i, cuts in enumerate(LATE_CUTS):
            @pl.when(ahead == late + i)
            def _():
                begin(late + i, (late + i) % SLOTS, cuts)
        return tall

    zero = jnp.zeros((SUBLANES, LANES), jnp.float32)
    half = edge // UNITS
    logits = [0.0] * UNITS
    edge_copy.wait()
    for k in range(depth):
        part = slice(k * UNIT, (k + 1) * UNIT)
        for q in range(UNITS):
            logits[q] += jnp.dot(edge_ref[q * half:(q + 1) * half, part], xt_ref[part, :], preferred_element_type=jnp.float32)
    tiles, hits = [], []
    for q in range(UNITS):
        tiles += tall_tiles(logits[q])
        hits += tall_hits(tall_ids, q * half, half // SUBLANES)
    tall = fold((tiles[0], zero, zero, zero), tiles, hits, None)
    tall = lax.fori_loop(0, late, body, tall)
    for i, cuts in enumerate(LATE_CUTS):
        tall = trip_step(late + i, (late + i) % SLOTS, tall, cuts)

    columns = {}
    for t in range(positions):
        row_max, exp_sum, weighted, picked = (state_ref[s, t] for s in range(4))
        top = jnp.max(row_max, axis=1, keepdims=True)
        drop = row_max - top
        scale = jnp.exp(drop)
        for s, v in enumerate((None, scale * exp_sum, scale * (weighted + drop * exp_sum), picked)):
            columns[s, t] = top if s == 0 else jnp.sum(v, axis=1, keepdims=True)

    row_max, exp_sum, weighted, picked = tall

    top = jnp.max(row_max, axis=0, keepdims=True)
    drop = row_max - top
    scale = jnp.exp(drop)
    flat = (top, jnp.sum(scale * exp_sum, axis=0, keepdims=True),
            jnp.sum(scale * (weighted + drop * exp_sum), axis=0, keepdims=True), jnp.sum(picked, axis=0, keepdims=True))
    for s, v in enumerate(flat):
        for t in range(positions):
            columns[s + 4, t] = jnp.sum(jnp.where(lane == t * batch + sub, v, 0.0), axis=1, keepdims=True)
    packed = zero
    for (s, t), v in columns.items():
        packed = jnp.where(lane == s * FIELD + t, v, packed)
    all_ref[me] = packed
    mine_ref[...] = packed

    pl.semaphore_wait(barrier, n - 1)
    copies = []
    for o in order:
        copy = pltpu.make_async_remote_copy(
            src_ref=mine_ref, dst_ref=all_ref.at[me], send_sem=send_sem.at[o], recv_sem=recv_sem.at[o],
            device_id=(group, peers[o]), device_id_type=MESH)
        copy.start()
        copies.append(copy)
    for copy in copies:
        copy.wait()


def combine(all_ref, logp_ref, norm_ref, ent_ref):
    tiles = [all_ref[d] for d in range(all_ref.shape[0])]
    parts = [[tile if s == 0 else pltpu.roll(tile, LANES - s * FIELD, 1) for s in range(first, first + 4)] for first in (0, 4) for tile in tiles]
    top = functools.reduce(jnp.maximum, [part[0] for part in parts])
    exp_sum = weighted = picked = jnp.zeros((SUBLANES, LANES), jnp.float32)
    for row_max, sums, products, found in parts:
        drop = row_max - top
        scale = jnp.exp(drop)
        exp_sum = exp_sum + scale * sums
        weighted = weighted + scale * (products + drop * sums)
        picked = picked + found
    log_sum = jnp.log(exp_sum)
    log_norm = top + log_sum
    logp_ref[...] = (picked - log_norm)[:, :logp_ref.shape[1]]
    norm_ref[...] = log_norm[:, :norm_ref.shape[1]]
    ent_ref[...] = (log_sum - weighted / exp_sum)[:, :ent_ref.shape[1]]


def solution(mesh):
    n = mesh.shape['tp']

    def per_device(hidden, draft_ids, norm_gain, head_w):
        batch, positions, dim = hidden.shape
        drafts = draft_ids.shape[1]
        rows = batch * positions
        cols = head_w.shape[1]
        x = hidden.transpose(1, 0, 2).reshape(rows, dim)
        gain = norm_gain.reshape(dim // LANES, LANES)
        vmem = pl.BlockSpec(memory_space=pltpu.VMEM)
        hbm = pl.BlockSpec(memory_space=pltpu.HBM)
        f32 = jnp.float32
        padded = pl.cdiv(rows, PACK) * PACK
        every = pl.pallas_call(
            functools.partial(score, n),
            out_shape=jax.ShapeDtypeStruct((n, SUBLANES, LANES), f32),
            in_specs=[hbm] * 4,
            out_specs=vmem,
            scratch_shapes=[
                pltpu.VMEM((rows, dim), jnp.bfloat16),
                pltpu.VMEM((batch, drafts), jnp.int32),
                pltpu.VMEM((dim // LANES, LANES), jnp.bfloat16),
                pltpu.VMEM((padded, dim), jnp.bfloat16),
                pltpu.VMEM((dim, LANES), jnp.bfloat16),
                pltpu.VMEM((SLOTS, TRIP, dim), jnp.bfloat16),
                pltpu.VMEM((cols % TRIP, dim), jnp.bfloat16),
                pltpu.VMEM((4, positions, SUBLANES, LANES), f32),
                pltpu.VMEM((SUBLANES, LANES), f32),
                pltpu.SemaphoreType.DMA((3,)),
                pltpu.SemaphoreType.DMA((SLOTS, max(CUTS, *LATE_CUTS))),
                pltpu.SemaphoreType.DMA,
                pltpu.SemaphoreType.DMA((n,)),
                pltpu.SemaphoreType.DMA((n,)),
            ],
            compiler_params=pltpu.CompilerParams(collective_id=0, has_side_effects=True, vmem_limit_bytes=SCORE_VMEM),
        )(*[pltpu.with_memory_space_constraint(v, pltpu.HBM) for v in (x, draft_ids, gain, head_w.T)])
        return pl.pallas_call(
            combine,
            out_shape=(jax.ShapeDtypeStruct((batch, drafts), jnp.float32),
                       jax.ShapeDtypeStruct((batch, positions), jnp.float32),
                       jax.ShapeDtypeStruct((batch, positions), jnp.float32)),
            in_specs=[vmem],
            out_specs=(vmem, vmem, vmem),
            compiler_params=pltpu.CompilerParams(vmem_limit_bytes=1024 * 1024),
        )(every)

    specs_in = (P('dp', None, None), P('dp', None), P(None), P(None, 'tp'))
    specs_out = (P('dp', None), P('dp', None), P('dp', None))
    return jax.shard_map(per_device, mesh=mesh, in_specs=specs_in, out_specs=specs_out, check_vma=False)
```

time: 47.8 us -> 47.6 us (level)
    pallas_call x3 -> x2, Pallas kernels: 47.1 us -> 46.8 us  [the longest x1 46.1 us: per_device(): pl.pallas_call(functools.partial(score, n), out_shape=jax.ShapeDtypeStruc...]
where the time goes in v5:
time: 47.6 us; the launch traced here: 47.5 us
  Pallas kernels  46.8 us (98%)
  between operations  0.64 us (1%)
    pallas_call x1, Pallas kernels, per_device(): pl.pallas_call(functools.partial(score, n), out_shape=jax.ShapeDtypeStruc...  46.1 us

profile of v5, /device:TPU:0, one launch (start us, length us, event | category | flops | bytes accessed | tf_op | source)
XLA Modules:
  0.0 47.5 jit_solution(4732350308573346631)
XLA Ops:
  0.6 46.1 %shard_map.67.all_ref = f32[8,8,128]{2,1,0:T(8,128)S(1)} custom-call(bf16[72,4096]{1,0:T(8,128)(2,1)} %bitcast.5, s32[8,8]{1,0:T(8,128)} %ids_hbm.1, bf16[32,128]{1,0:T(8,128)(2,1)} %bitcast.6, bf16[16032,4096]{1,0:T(8,128)(2,1)} %bitcast.3.w_hbm), custom_call_target="tpu_custom_call" | custom-call | tf_op jit(solution)/shard_map/pallas_call | solution.py:247
  46.7 0.7 %shard_map.68 = (f32[8,8]{1,0:T(8,128)}, f32[8,9]{1,0:T(8,128)}, f32[8,9]{1,0:T(8,128)}) custom-call(f32[8,8,128]{2,1,0:T(8,128)S(1)} %shard_map.67.all_ref), custom_call_target="tpu_custom_call" | custom-call | tf_op jit(solution)/shard_map/pallas_call | solution.py:270

commit v6 on v5

--- a/solution.py
+++ b/solution.py
@@ -14,12 +14,12 @@
 UNIT = 256
 PACK = 16
 HELD = 256
-MOVED = 304
+MOVED = 272
 UNITS = 2
 TRIP = UNITS * (HELD + MOVED)
-SLOTS = 4
-CUTS = 2
-LATE_CUTS = (4, 4)
+SLOTS = 3
+CUTS = (8, 8)
+LATE_CUTS = ((6, 5, 5), (6, 5, 3, 2))
 SCORE_VMEM = 46 * 1024 * 1024
 FIELD = 16
 
@@ -69,11 +69,11 @@
 
     def fetch(trip, slot, cuts, c):
         start = pl.multiple_of(edge + trip * TRIP, SUBLANES)
-        part = pl.ds(c * (dim // cuts), dim // cuts)
+        part = pl.ds(sum(cuts[:c]) * UNIT, cuts[c] * UNIT)
         return pltpu.make_async_copy(w_hbm.at[pl.ds(start, TRIP), part], w_ref.at[slot, :, part], w_sem.at[slot, c])
 
     def begin(trip, slot, cuts=CUTS):
-        for c in range(cuts):
+        for c in range(len(cuts)):
             fetch(trip, slot, cuts, c).start(priority=1)
 
     inputs = [pltpu.make_async_copy(src, dst, in_sem.at[i])
@@ -121,8 +121,9 @@
     def trip_step(trip, slot, tall, cuts=CUTS):
         moved, held = [0.0] * UNITS, [0.0] * UNITS
         for k in range(depth):
-            if k % (depth // cuts) == 0:
-                fetch(trip, slot, cuts, k // (depth // cuts)).wait()
+            for c in range(len(cuts)):
+                if k == sum(cuts[:c]):
+                    fetch(trip, slot, cuts, c).wait()
             part = slice(k * UNIT, (k + 1) * UNIT)
             for q in range(UNITS):
                 top = q * (HELD + MOVED)
@@ -260,7 +261,7 @@
                 pltpu.VMEM((4, positions, SUBLANES, LANES), f32),
                 pltpu.VMEM((SUBLANES, LANES), f32),
                 pltpu.SemaphoreType.DMA((3,)),
-                pltpu.SemaphoreType.DMA((SLOTS, max(CUTS, *LATE_CUTS))),
+                pltpu.SemaphoreType.DMA((SLOTS, max(map(len, (CUTS, *LATE_CUTS))))),
                 pltpu.SemaphoreType.DMA,
                 pltpu.SemaphoreType.DMA((n,)),
                 pltpu.SemaphoreType.DMA((n,)),

time: 47.6 us -> 47.5 us (level)
  no operation moved by 1% of the time
where the time goes in v6:
time: 47.5 us; the launch traced here: 47.4 us
  Pallas kernels  46.7 us (98%)
  between operations  0.64 us (1%)
    pallas_call x1, Pallas kernels, per_device(): pl.pallas_call(functools.partial(score, n), out_shape=jax.ShapeDtypeStruc...  46 us

profile of v6, /device:TPU:0, one launch (start us, length us, event | category | flops | bytes accessed | tf_op | source)
XLA Modules:
  0.0 47.4 jit_solution(16287580386437282054)
XLA Ops:
  0.6 46.0 %shard_map.67.all_ref = f32[8,8,128]{2,1,0:T(8,128)S(1)} custom-call(bf16[72,4096]{1,0:T(8,128)(2,1)} %bitcast.5, s32[8,8]{1,0:T(8,128)} %ids_hbm.1, bf16[32,128]{1,0:T(8,128)(2,1)} %bitcast.6, bf16[16032,4096]{1,0:T(8,128)(2,1)} %bitcast.3.w_hbm), custom_call_target="tpu_custom_call" | custom-call | tf_op jit(solution)/shard_map/pallas_call | solution.py:248
  46.6 0.7 %shard_map.68 = (f32[8,8]{1,0:T(8,128)}, f32[8,9]{1,0:T(8,128)}, f32[8,9]{1,0:T(8,128)}) custom-call(f32[8,8,128]{2,1,0:T(8,128)S(1)} %shard_map.67.all_ref), custom_call_target="tpu_custom_call" | custom-call | tf_op jit(solution)/shard_map/pallas_call | solution.py:271

commit v7 on v6

--- a/solution.py
+++ b/solution.py
@@ -192,12 +192,12 @@
     scale = jnp.exp(drop)
     flat = (top, jnp.sum(scale * exp_sum, axis=0, keepdims=True),
             jnp.sum(scale * (weighted + drop * exp_sum), axis=0, keepdims=True), jnp.sum(picked, axis=0, keepdims=True))
-    for s, v in enumerate(flat):
+    packed = zero
+    for s in range(4):
+        spread = zero
         for t in range(positions):
-            columns[s + 4, t] = jnp.sum(jnp.where(lane == t * batch + sub, v, 0.0), axis=1, keepdims=True)
-    packed = zero
-    for (s, t), v in columns.items():
-        packed = jnp.where(lane == s * FIELD + t, v, packed)
+            spread = jnp.where(lane == t * batch + sub, columns[s, t], spread)
+        packed = jnp.where(sub == s, flat[s], jnp.where(sub == s + 4, jnp.sum(spread, axis=0, keepdims=True), packed))
     all_ref[me] = packed
     mine_ref[...] = packed
 
@@ -214,21 +214,26 @@
 
 
 def combine(all_ref, logp_ref, norm_ref, ent_ref):
-    tiles = [all_ref[d] for d in range(all_ref.shape[0])]
-    parts = [[tile if s == 0 else pltpu.roll(tile, LANES - s * FIELD, 1) for s in range(first, first + 4)] for first in (0, 4) for tile in tiles]
-    top = functools.reduce(jnp.maximum, [part[0] for part in parts])
-    exp_sum = weighted = picked = jnp.zeros((SUBLANES, LANES), jnp.float32)
+    parts = [[all_ref[:, s, :] for s in range(first, first + 4)] for first in (0, 4)]
+    top = functools.reduce(jnp.maximum, [jnp.max(part[0], axis=0, keepdims=True) for part in parts])
+    exp_sum = weighted = picked = jnp.zeros((all_ref.shape[0], LANES), jnp.float32)
     for row_max, sums, products, found in parts:
         drop = row_max - top
         scale = jnp.exp(drop)
         exp_sum = exp_sum + scale * sums
         weighted = weighted + scale * (products + drop * sums)
         picked = picked + found
+    exp_sum, weighted, picked = (jnp.sum(v, axis=0, keepdims=True) for v in (exp_sum, weighted, picked))
     log_sum = jnp.log(exp_sum)
     log_norm = top + log_sum
-    logp_ref[...] = (picked - log_norm)[:, :logp_ref.shape[1]]
-    norm_ref[...] = log_norm[:, :norm_ref.shape[1]]
-    ent_ref[...] = (log_sum - weighted / exp_sum)[:, :ent_ref.shape[1]]
+    lane = lax.broadcasted_iota(jnp.int32, (SUBLANES, LANES), 1)
+    sub = lax.broadcasted_iota(jnp.int32, (SUBLANES, LANES), 0)
+    for ref, values in ((logp_ref, picked - log_norm), (norm_ref, log_norm), (ent_ref, log_sum - weighted / exp_sum)):
+        out = jnp.zeros((SUBLANES, LANES), jnp.float32)
+        for t in range(ref.shape[1]):
+            column = jnp.sum(jnp.where(lane == t * SUBLANES + sub, values, 0.0), axis=1, keepdims=True)
+            out = jnp.where(lane == t, column, out)
+        ref[...] = out[:, :ref.shape[1]]
 
 
 def solution(mesh):

time: 47.5 us -> 47.4 us (level)
  no operation moved by 1% of the time
where the time goes in v7:
time: 47.4 us
  Pallas kernels  46.7 us (99%)
  between operations  0.64 us (1%)
    pallas_call x1, Pallas kernels, per_device(): pl.pallas_call(functools.partial(score, n), out_shape=jax.ShapeDtypeStruc...  46 us

profile of v7, /device:TPU:0, one launch (start us, length us, event | category | flops | bytes accessed | tf_op | source)
XLA Modules:
  0.0 47.4 jit_solution(9655775718960223504)
XLA Ops:
  0.6 46.0 %shard_map.67.all_ref = f32[8,8,128]{2,1,0:T(8,128)S(1)} custom-call(bf16[72,4096]{1,0:T(8,128)(2,1)} %bitcast.5, s32[8,8]{1,0:T(8,128)} %ids_hbm.1, bf16[32,128]{1,0:T(8,128)(2,1)} %bitcast.6, bf16[16032,4096]{1,0:T(8,128)(2,1)} %bitcast.3.w_hbm), custom_call_target="tpu_custom_call" | custom-call | tf_op jit(solution)/shard_map/pallas_call | solution.py:253
  46.6 0.7 %shard_map.68 = (f32[8,8]{1,0:T(8,128)}, f32[8,9]{1,0:T(8,128)}, f32[8,9]{1,0:T(8,128)}) custom-call(f32[8,8,128]{2,1,0:T(8,128)S(1)} %shard_map.67.all_ref), custom_call_target="tpu_custom_call" | custom-call | tf_op jit(solution)/shard_map/pallas_call | solution.py:276
